TPU v7x, 32 devices: a whole 2x2x4 slice. The times are simulated.
32 devices in a mesh: mem: 4 (over x, core), slab: 8 (over z, y).
Axes of the slice: x: 2, y: 2, z: 4, core: 2. Of those that a mesh axis runs over, the one named last changes fastest.
Arguments:
- anomalies: bfloat16 [8, 4096, 4096], P('mem', 'slab'), may hold values from -2.390625 to 2.390625
- increment: float32 [4096, 4096], P('slab'), may hold values from -6 to 6
- spectrum: float32 [4096, 4096], P(None, 'slab'), may hold values from 0.01 to 2, as said below
Outputs:
- product: float32 [4096, 4096], P('slab')
Inputs may be any that keep to these rules, and one draw needn't show every extreme that they name: spectrum[k, l] equals spectrum[(4096 - k) % 4096, (4096 - l) % 4096], and is positive.
All inputs are finite; a program needn't handle non-finite values.
Results may differ from a plain program's by a relative error of at most 0.0003.
Values sent between devices are 32-bit elements; how exact they have to be, the bound alone decides.
No kernel may reach another device: no remote copies, remote signals or barrier semaphores. Data moves between devices by JAX's collectives and lax.ppermute only.
A program may use at most 192 MiB of HBM per device.

v0:
```python
import math

import jax
import jax.numpy as jnp
from jax import lax
from jax.sharding import PartitionSpec as P


def dft_tables(length, sign):
    first = 1 << (length.bit_length() - 1) // 2
    second = length // first
    index_a = jnp.arange(first, dtype=jnp.int32)
    index_b = jnp.arange(second, dtype=jnp.int32)
    angle_first = (
        2.0 * math.pi / first * (index_a[:, None] * index_a[None, :] % first).astype(jnp.float32)
    )
    angle_twist = (
        2.0 * math.pi / length * (index_a[:, None] * index_b[None, :] % length).astype(jnp.float32)
    )
    angle_second = (
        2.0 * math.pi / second * (index_b[:, None] * index_b[None, :] % second).astype(jnp.float32)
    )
    return (
        first,
        jnp.cos(angle_first),
        sign * jnp.sin(angle_first),
        jnp.cos(angle_twist),
        sign * jnp.sin(angle_twist),
        jnp.cos(angle_second),
        sign * jnp.sin(angle_second),
    )


def complex_section(form, real_part, imag_part, mat_cos, mat_sin):
    highest = lax.Precision.HIGHEST
    out_real = jnp.einsum(form, real_part, mat_cos, precision=highest)
    out_real = out_real - jnp.einsum(form, imag_part, mat_sin, precision=highest)
    out_imag = jnp.einsum(form, real_part, mat_sin, precision=highest)
    out_imag = out_imag + jnp.einsum(form, imag_part, mat_cos, precision=highest)
    return (out_real, out_imag)


def transform(real_part, imag_part, factors, along_last):
    first, first_cos, first_sin, twist_cos, twist_sin, second_cos, second_sin = factors
    shape = real_part.shape
    if along_last:
        blocked = (shape[0], shape[1], first, shape[2] // first)
        form_one, form_two = ("mrab,ac->mrcb", "mrcb,bd->mrdc")
        tw_cos, tw_sin = (twist_cos, twist_sin)
    else:
        blocked = (shape[0], first, shape[1] // first, shape[2])
        form_one, form_two = ("mabk,ac->mcbk", "mcbk,bd->mdck")
        tw_cos, tw_sin = (twist_cos[:, :, None], twist_sin[:, :, None])
    real_part = real_part.reshape(blocked)
    imag_part = imag_part.reshape(blocked)
    step_real, step_imag = complex_section(form_one, real_part, imag_part, first_cos, first_sin)
    twist_real = step_real * tw_cos - step_imag * tw_sin
    twist_imag = step_real * tw_sin + step_imag * tw_cos
    out_real, out_imag = complex_section(form_two, twist_real, twist_imag, second_cos, second_sin)
    out_real = out_real.reshape(shape)
    out_imag = out_imag.reshape(shape)
    return (out_real, out_imag)


def per_device(anomalies, increment, spectrum):
    col_count = anomalies.shape[2]
    row_total = spectrum.shape[0]
    forward_y = dft_tables(col_count, -1.0)
    inverse_y = dft_tables(col_count, 1.0)
    forward_x = dft_tables(row_total, -1.0)
    inverse_x = dft_tables(row_total, 1.0)
    scaled = spectrum * (1.0 / (row_total * col_count))
    fields = anomalies * increment[None]
    wave_real, wave_imag = transform(fields[0::2], fields[1::2], forward_y, True)
    part_real, part_imag = transform(
        lax.all_to_all(wave_real, "slab", split_axis=2, concat_axis=1, tiled=True),
        lax.all_to_all(wave_imag, "slab", split_axis=2, concat_axis=1, tiled=True),
        forward_x,
        False,
    )
    part_real = part_real * scaled[None]
    part_imag = part_imag * scaled[None]
    part_real, part_imag = transform(part_real, part_imag, inverse_x, False)
    back_real = lax.all_to_all(part_real, "slab", split_axis=1, concat_axis=2, tiled=True)
    back_imag = lax.all_to_all(part_imag, "slab", split_axis=1, concat_axis=2, tiled=True)
    even_part, odd_part = transform(back_real, back_imag, inverse_y, True)
    total = jnp.sum(anomalies[0::2] * even_part + anomalies[1::2] * odd_part, axis=0)
    return lax.psum(total, "mem")


def solution(mesh):
    placed = (P("mem", "slab", None), P("slab", None), P(None, "slab"))
    return jax.shard_map(
        per_device, mesh=mesh, in_specs=placed, out_specs=P("slab", None), check_vma=False
    )
```

profile of v0, /device:TPU:0, one launch (start us, length us, event | category | flops | bytes accessed | tf_op | source)
XLA Modules:
  0.0 1516.1 jit_solution(14172679125190159585)
XLA Ops:
  6.7 12.0 copy.122
  18.6 9.0 copy.124
  27.7 12.1 convert_multiply_fusion
  39.8 6.9 fusion.324
  46.7 13.2 fusion.65
  59.9 13.3 fusion.67
  73.2 13.3 fusion.69
  86.5 24.8 %fusion.6 = (f32[512,64,64]{0,1,2:T(8,128)}, f32[512,64,64]{0,1,2:T(8,128)}) fusion(f32[64,64]{0,1:T(8,128)S(1)} %get-tuple-element.17, f32[64,64]{0,1:T(8,128)S(1)} %get-tuple-element.18, f32[64,512,64]{1,0,2:T(8,128)} %fusion.69, f32[64,512,64]{1,0,2:T(8,128)} %fusion.65, f32[64,512,64]{1,0,2:T(8,128)} %fusion.67, f32[512,64,64]{0,2,1:T(8,128)} %bitcast.203), kind=kOutput, calls=%fused_computation.17 | convolution fusion | flops 1627447296 | bytes 50364416 | tf_op jit(solution)/shard_map/mrab,ac->mrcb/dot_general | solution.py:36
  111.3 16.5 %fusion.57 = f32[64,512,64]{1,0,2:T(8,128)S(1)} fusion(f32[512,64,64]{0,1,2:T(8,128)} %get-tuple-element.12), kind=kOutput, calls=%fused_computation.78 | convolution fusion | flops 1610670080 | bytes 16777216 | tf_op jit(solution)/shard_map/mrcb,bd->mrdc/dot_general | solution.py:39
  127.8 12.0 add_bitcast_fusion.1
  139.8 5.1 copy.137
  144.8 22.8 %copy.138 = f32[1,512,4096]{1,0,2:T(1,128)} copy(f32[1,512,4096]{1,2,0:T(8,128)S(1)} %bitcast.204) | data formatting | bytes 16777216 | tf_op jit(solution)/shard_map/reshape | solution.py:61
  167.6 7.6 all-to-all-start.1
  175.2 16.3 %fusion.59 = f32[64,512,64]{1,0,2:T(8,128)S(1)} fusion(f32[512,64,64]{0,1,2:T(8,128)} %get-tuple-element.12), kind=kOutput, calls=%fused_computation.80 | convolution fusion | flops 1610674176 | bytes 16777216 | tf_op jit(solution)/shard_map/mrcb,bd->mrdc/dot_general | solution.py:37
  191.6 17.2 %subtract_bitcast_fusion.1 = f32[1,512,64,64]{1,2,3,0:T(8,128)S(1)} fusion(f32[64,512,64]{1,0,2:T(8,128)S(1)} %fusion.59, f32[512,64,64]{0,1,2:T(8,128)} %get-tuple-element.11), kind=kOutput, calls=%fused_computation.29 | convolution fusion | flops 1612767232 | bytes 25165824 | tf_op jit(solution)/shard_map/mrcb,bd->mrdc/dot_general | solution.py:36
  213.7 22.8 %copy.132 = f32[1,512,4096]{1,0,2:T(1,128)} copy(f32[1,512,4096]{1,2,0:T(8,128)S(1)} %bitcast.205) | data formatting | bytes 16777216 | tf_op jit(solution)/shard_map/reshape | solution.py:60
  236.5 121.8 %all-to-all-done.1 = f32[1,512,4096]{1,0,2:T(1,128)} async-done(((f32[1,512,4096]{1,0,2:T(1,128)}), f32[1,512,4096]{1,0,2:T(1,128)}, u32[]{:S(2)}, u32[]{:S(2)}) %all-to-all-start.1) | async-done | bytes 8388640 | tf_op jit(solution)/shard_map/all_to_all | solution.py:77
  358.3 5.2 all-to-all-start
  363.6 7.6 copy.176
  371.2 9.2 copy.139
  380.4 17.8 %fusion.49 = f32[64,64,512]{2,0,1:T(8,128)} fusion(f32[64,64,512]{2,1,0:T(8,128)} %bitcast.190), kind=kOutput, calls=%fused_computation.70 | convolution fusion | flops 1610670080 | bytes 16777216 | tf_op jit(solution)/shard_map/mabk,ac->mcbk/dot_general | solution.py:39
  398.2 13.5 fusion.51
  411.7 134.0 %all-to-all-done = f32[1,512,4096]{1,0,2:T(1,128)} async-done(((f32[1,512,4096]{1,0,2:T(1,128)}), f32[1,512,4096]{1,0,2:T(1,128)}, u32[]{:S(2)}, u32[]{:S(2)}) %all-to-all-start) | async-done | bytes 8388640 | tf_op jit(solution)/shard_map/all_to_all | solution.py:76
  545.7 7.6 copy.175
  553.4 9.1 copy.133
  562.5 18.1 %fusion.55 = f32[64,64,512]{2,0,1:T(8,128)} fusion(f32[64,64,512]{2,1,0:T(8,128)} %bitcast.196), kind=kOutput, calls=%fused_computation.76 | convolution fusion | flops 1610670080 | bytes 16777216 | tf_op jit(solution)/shard_map/mabk,ac->mcbk/dot_general | solution.py:36
  580.6 24.6 %multiply_subtract_fusion.1 = (f32[64,64,512]{2,0,1:T(8,128)}, f32[64,64,512]{2,0,1:T(8,128)}) fusion(f32[64,64]{0,1:T(8,128)S(1)} %get-tuple-element.17, f32[64,64]{0,1:T(8,128)S(1)} %get-tuple-element.18, f32[64,64,512]{2,0,1:T(8,128)} %fusion.49, f32[64,64,512]{2,0,1:T(8,128)} %fusion.55, f32[64,64,512]{2,0,1:T(8,128)} %fusion.51, ...), kind=kOutput, calls=%fused_computation.27 | convolution fusion | flops 1627451392 | bytes 50364416 | tf_op jit(solution)/shard_map/mabk,ac->mcbk/dot_general | solution.py:38
  605.2 18.4 %fusion.43 = f32[64,64,512]{2,0,1:T(8,128)} fusion(f32[64,64,512]{2,0,1:T(8,128)} %get-tuple-element.10), kind=kOutput, calls=%fused_computation.64 | convolution fusion | flops 1610674176 | bytes 16777216 | tf_op jit(solution)/shard_map/mcbk,bd->mdck/dot_general | solution.py:37
  623.6 12.5 fusion.41
  636.1 15.6 %fusion.77 = f32[64,64,512]{2,0,1:T(8,128)} fusion(f32[64,64,512]{2,0,1:T(8,128)} %fusion.43, f32[64,64,512]{2,0,1:T(8,128)S(1)} %bitcast.183), kind=kOutput, calls=%fused_computation.94 | convolution fusion | flops 1612767232 | bytes 25165824 | tf_op jit(solution)/shard_map/mcbk,bd->mdck/dot_general | solution.py:36
  651.8 11.5 copy.145
  663.3 13.8 fusion.80
  677.1 11.5 copy.149
  688.6 13.8 bitcast_multiply_fusion.6
  702.3 13.2 fusion.33
  715.6 13.3 fusion.35
  728.8 13.2 fusion.39
  742.1 24.8 %multiply_subtract_fusion = (f32[64,64,512]{2,0,1:T(8,128)}, f32[64,64,512]{2,0,1:T(8,128)}) fusion(f32[64,64]{0,1:T(8,128)S(1)} %fusion.152, f32[64,64]{0,1:T(8,128)S(1)} %get-tuple-element.18, f32[64,64,512]{2,0,1:T(8,128)} %fusion.33, f32[64,64,512]{2,0,1:T(8,128)} %fusion.39, f32[64,64,512]{2,0,1:T(8,128)} %fusion.35, f32[64,64,512]{2,1,0:T(8,128)} %bitcast.186), kind=kOutput, calls=%fused_computation.25 | convolution fusion | flops 1627447296 | bytes 50364416 | tf_op jit(solution)/shard_map/mabk,ac->mcbk/dot_general | solution.py:38
  766.9 16.5 %fusion.25 = f32[64,64,512]{2,0,1:T(8,128)S(1)} fusion(f32[64,64,512]{2,0,1:T(8,128)} %get-tuple-element.8), kind=kOutput, calls=%fused_computation.46 | convolution fusion | flops 1610670080 | bytes 16777216 | tf_op jit(solution)/shard_map/mcbk,bd->mdck/dot_general | solution.py:39
  783.4 12.0 fusion.86
  800.5 22.8 %copy.162 = f32[1,4096,512]{2,0,1:T(1,128)} copy(f32[1,4096,512]{2,1,0:T(8,128)S(1)} %bitcast.208) | data formatting | bytes 16777216 | tf_op jit(solution)/shard_map/reshape | solution.py:61
  823.3 5.2 all-to-all-start.3
  828.5 16.3 %fusion.27 = f32[64,64,512]{2,0,1:T(8,128)S(1)} fusion(f32[64,64,512]{2,0,1:T(8,128)} %get-tuple-element.8), kind=kOutput, calls=%fused_computation.48 | convolution fusion | flops 1610670080 | bytes 16777216 | tf_op jit(solution)/shard_map/mcbk,bd->mdck/dot_general | solution.py:37
  844.8 17.2 %fusion.83 = f32[64,64,512]{2,0,1:T(8,128)S(1)} fusion(f32[64,64,512]{2,0,1:T(8,128)S(1)} %fusion.27, f32[64,64,512]{2,0,1:T(8,128)} %get-tuple-element.7), kind=kOutput, calls=%fused_computation.96 | convolution fusion | flops 1612767232 | bytes 25165824 | tf_op jit(solution)/shard_map/mcbk,bd->mdck/dot_general | solution.py:36
  866.9 22.8 %copy.156 = f32[1,4096,512]{2,0,1:T(1,128)} copy(f32[1,4096,512]{2,1,0:T(8,128)S(1)} %bitcast.209) | data formatting | bytes 16777216 | tf_op jit(solution)/shard_map/reshape | solution.py:60
  889.7 120.7 %all-to-all-done.3 = f32[1,4096,512]{2,0,1:T(1,128)} async-done(((f32[1,4096,512]{2,0,1:T(1,128)}), f32[1,4096,512]{2,0,1:T(1,128)}, u32[]{:S(2)}, u32[]{:S(2)}) %all-to-all-start.3) | async-done | bytes 8388640 | tf_op jit(solution)/shard_map/all_to_all | solution.py:85
  1015.4 7.6 copy.178
  1023.0 9.4 copy.163
  1032.4 17.8 %fusion.17 = f32[64,512,64]{1,0,2:T(8,128)} fusion(f32[512,64,64]{0,2,1:T(8,128)} %bitcast.192), kind=kOutput, calls=%fused_computation.38 | convolution fusion | flops 1610670080 | bytes 16777216 | tf_op jit(solution)/shard_map/mrab,ac->mrcb/dot_general | solution.py:39
  1050.2 13.4 fusion.19
  1063.5 134.1 %all-to-all-done.2 = f32[1,4096,512]{2,0,1:T(1,128)} async-done(((f32[1,4096,512]{2,0,1:T(1,128)}), f32[1,4096,512]{2,0,1:T(1,128)}, u32[]{:S(2)}, u32[]{:S(2)}) %all-to-all-start.2) | async-done | bytes 8388640 | tf_op jit(solution)/shard_map/all_to_all | solution.py:84
  1197.6 7.6 copy.177
  1205.2 9.2 copy.157
  1214.4 18.1 %fusion.21 = f32[64,512,64]{1,0,2:T(8,128)} fusion(f32[512,64,64]{0,2,1:T(8,128)} %bitcast.194), kind=kOutput, calls=%fused_computation.42 | convolution fusion | flops 1610670080 | bytes 16777216 | tf_op jit(solution)/shard_map/mrab,ac->mrcb/dot_general | solution.py:38
  1232.4 24.5 %fusion.2 = (f32[512,64,64]{0,1,2:T(8,128)}, f32[512,64,64]{0,1,2:T(8,128)}) fusion(f32[64,64]{0,1:T(8,128)S(1)} %fusion.152, f32[64,64]{0,1:T(8,128)S(1)} %get-tuple-element.18, f32[64,512,64]{1,0,2:T(8,128)} %fusion.21, f32[64,512,64]{1,0,2:T(8,128)} %fusion.17, f32[64,512,64]{1,0,2:T(8,128)} %fusion.19, f32[512,64,64]{0,2,1:T(8,128)} %bitcast.195), kind=kOutput, calls=%fused_computation.7 | convolution fusion | flops 1627447296 | bytes 50364416 | tf_op jit(solution)/shard_map/mrab,ac->mrcb/dot_general | solution.py:36
  1257.0 17.0 %fusion.11 = f32[64,512,64]{1,0,2:T(8,128)S(1)} fusion(f32[512,64,64]{0,1,2:T(8,128)} %get-tuple-element.6), kind=kOutput, calls=%fused_computation.32 | convolution fusion | flops 1610670080 | bytes 16777216 | tf_op jit(solution)/shard_map/mrcb,bd->mrdc/dot_general | solution.py:37
  1274.0 13.5 fusion.9
  1287.5 13.7 subtract_bitcast_fusion
  1301.3 11.7 copy.169
  1313.0 15.6 %add_bitcast_fusion = f32[1,512,64,64]{1,2,3,0:T(8,128)} fusion(f32[64,512,64]{1,0,2:T(8,128)} %fusion.9, f32[512,64,64]{0,1,2:T(8,128)S(1)} %bitcast.181), kind=kOutput, calls=%fused_computation.22 | convolution fusion | flops 1612767232 | bytes 25165824 | tf_op jit(solution)/shard_map/mrcb,bd->mrdc/dot_general | solution.py:38
  1328.6 11.7 copy.173
  1340.3 7.5 fusion
  1347.9 152.2 %all-reduce.2.cloned.1.call-done = f32[512,4096]{0,1:T(8,128)} async-done(((f32[512,4096]{0,1:T(8,128)}), f32[512,4096]{0,1:T(8,128)}) %all-reduce.2.cloned.1.call-update) | async-done | bytes 8388624 | tf_op jit(solution)/shard_map/psum | solution.py:88
  1500.1 8.9 copy.174
  (44 shorter events, 20.1 us)
Async XLA Ops:
  46.7 26.6 %copy-start.6 = (f32[1,512,4096]{1,2,0:T(8,128)}, f32[1,512,4096]{1,2,0:T(8,128)S(1)}, u32[]{:S(2)}) copy-start(f32[1,512,4096]{1,2,0:T(8,128)S(1)} %get-tuple-element.14) | copy-start | bytes 25165828
  111.3 16.5 %copy-start = (f32[512,64,64]{0,1,2:T(8,128)S(1)}, f32[512,64,64]{0,1,2:T(8,128)}, u32[]{:S(2)}) copy-start(f32[512,64,64]{0,1,2:T(8,128)} %get-tuple-element.11) | copy-start | bytes 25165828
  167.6 190.7 %all-to-all-start.1 = ((f32[1,512,4096]{1,0,2:T(1,128)}), f32[1,512,4096]{1,0,2:T(1,128)}, u32[]{:S(2)}, u32[]{:S(2)}) async-start(f32[1,512,4096]{1,0,2:T(1,128)} %copy.138), calls=%async_computation.1 | async-start | bytes 16777216 | tf_op jit(solution)/shard_map/all_to_all | solution.py:77
  358.3 187.4 %all-to-all-start = ((f32[1,512,4096]{1,0,2:T(1,128)}), f32[1,512,4096]{1,0,2:T(1,128)}, u32[]{:S(2)}, u32[]{:S(2)}) async-start(f32[1,512,4096]{1,0,2:T(1,128)} %copy.132), calls=%async_computation | async-start | bytes 16777216 | tf_op jit(solution)/shard_map/all_to_all | solution.py:76
  380.4 17.8 %copy-start.2 = (f32[1,8,512,512]{3,2,1,0:T(8,128)S(1)}, f32[1,8,512,512]{3,2,1,0:T(8,128)}, u32[]{:S(2)}) copy-start(f32[1,8,512,512]{3,2,1,0:T(8,128)} %copy.139) | copy-start | bytes 25165828
  605.2 18.4 %copy-start.5 = (f32[64,64,512]{2,0,1:T(8,128)S(1)}, f32[64,64,512]{2,0,1:T(8,128)}, u32[]{:S(2)}) copy-start(f32[64,64,512]{2,0,1:T(8,128)} %get-tuple-element.10) | copy-start | bytes 25165828
  605.2 30.9 %slice-start.2 = ((s8[8388608]{0:T(1024)(128)(4,1)}), s8[4194304]{0:T(1024)(128)(4,1)S(1)}, s32[]{:S(2)}) async-start(s8[8388608]{0:T(1024)(128)(4,1)} %bitcast.182), calls=%async_computation.7 | async-start | bytes 8388608
  623.6 12.5 slice-start.3
  702.3 26.5 %slice-start.4 = ((s8[8388608]{0:T(1024)(128)(4,1)}), s8[4194304]{0:T(1024)(128)(4,1)S(1)}, s32[]{:S(2)}) async-start(s8[8388608]{0:T(1024)(128)(4,1)} %bitcast.187), calls=%async_computation.9 | async-start | bytes 8388608
  715.6 13.3 slice-start.5
  766.9 16.5 %copy-start.1 = (f32[64,64,512]{2,0,1:T(8,128)S(1)}, f32[64,64,512]{2,0,1:T(8,128)}, u32[]{:S(2)}) copy-start(f32[64,64,512]{2,0,1:T(8,128)} %get-tuple-element.7) | copy-start | bytes 25165828
  823.3 187.2 %all-to-all-start.3 = ((f32[1,4096,512]{2,0,1:T(1,128)}), f32[1,4096,512]{2,0,1:T(1,128)}, u32[]{:S(2)}, u32[]{:S(2)}) async-start(f32[1,4096,512]{2,0,1:T(1,128)} %copy.162), calls=%async_computation.3 | async-start | bytes 16777216 | tf_op jit(solution)/shard_map/all_to_all | solution.py:85
  1010.4 187.2 %all-to-all-start.2 = ((f32[1,4096,512]{2,0,1:T(1,128)}), f32[1,4096,512]{2,0,1:T(1,128)}, u32[]{:S(2)}, u32[]{:S(2)}) async-start(f32[1,4096,512]{2,0,1:T(1,128)} %copy.156), calls=%async_computation.2 | async-start | bytes 16777216 | tf_op jit(solution)/shard_map/all_to_all | solution.py:84
  1015.4 484.7 %all-reduce.2.cloned.1.call-start = ((), (), s32[]{:S(2)}) async-start(), calls=%async_computation.4 | async-start | bytes 16777216 | tf_op jit(solution)/shard_map/psum | solution.py:88
  1032.4 17.8 %copy-start.3 = (f32[1,512,8,512]{1,3,2,0:T(8,128)S(1)}, f32[1,512,8,512]{1,3,2,0:T(8,128)}, u32[]{:S(2)}) copy-start(f32[1,512,8,512]{1,3,2,0:T(8,128)} %copy.163) | copy-start | bytes 25165828
  1256.9 17.0 %copy-start.4 = (f32[512,64,64]{0,1,2:T(8,128)S(1)}, f32[512,64,64]{0,1,2:T(8,128)}, u32[]{:S(2)}) copy-start(f32[512,64,64]{0,1,2:T(8,128)} %get-tuple-element.6) | copy-start | bytes 25165828
  1256.9 30.6 %slice-start = ((s8[8388608]{0:T(1024)(128)(4,1)}), s8[4194304]{0:T(1024)(128)(4,1)S(1)}, s32[]{:S(2)}) async-start(s8[8388608]{0:T(1024)(128)(4,1)} %bitcast.180), calls=%async_computation.5 | async-start | bytes 8388608
  1274.0 13.5 slice-start.1
  1301.3 39.0 %slice-start.6 = ((s8[8388608]{0:T(1024)(128)(4,1)}), s8[4194304]{0:T(1024)(128)(4,1)S(1)}, s32[]{:S(2)}) async-start(s8[8388608]{0:T(1024)(128)(4,1)} %bitcast.200), calls=%async_computation.11 | async-start | bytes 8388608
  1313.0 27.3 %slice-start.7 = ((s8[8388608]{0:T(1024)(128)(4,1)}), s8[4194304]{0:T(1024)(128)(4,1)S(1)}, s32[]{:S(2)}) async-start(s8[8388608]{0:T(1024)(128)(4,1)} %bitcast.200), calls=%async_computation.12 | async-start | bytes 8388608
  1328.6 11.7 copy-start.7
Sparse Core Ops, SparseCore 0:
  1348.0 152.0 all-reduce.1
where the time goes:
time: 1520 us
  waiting for transfers between devices  663 us (44%)
  matrix products  521 us (34%)
  local copies, waits for them, and re-layouts  261 us (17%)
  other arithmetic  33.7 us (2%)
  starting transfers between devices  23 us (2%)
    psum x1, waiting for transfers between devices, per_device(): return lax.psum(total, 'mem')  152 us
    dot_general x8, matrix products, complex_section(): out_real = jnp.einsum(form, real_part, mat_cos, precision=highest)  144 us
    dot_general x8, matrix products, complex_section(): out_imag = jnp.einsum(form, real_part, mat_sin, precision=highest)  134 us
    all_to_all x1, waiting for transfers between devices, per_device(): lax.all_to_all(part_real, 'slab', split_axis=1, concat_axis=2, tiled=True)  134 us
    all_to_all x1, waiting for transfers between devices, per_device(): lax.all_to_all(wave_real, 'slab', split_axis=2, concat_axis=1, tiled=True)  134 us
    all_to_all x1, waiting for transfers between devices, per_device(): lax.all_to_all(wave_imag, 'slab', split_axis=2, concat_axis=1, tiled=True)  122 us
    dot_general x8, matrix products, complex_section(): jnp.einsum(form, imag_part, mat_sin, precision=highest)  121 us
    dot_general x8, matrix products, complex_section(): jnp.einsum(form, imag_part, mat_cos, precision=highest)  121 us
  transfers between devices with their start and end apart: 5, of which 5 were waited for; matrix products, arithmetic and copies ran while one was open for 14% of the time, Pallas kernels for 0%

commit v1 on v0

v1 whole, which is shorter than its diff:
```python
import math

import jax
import jax.numpy as jnp
from jax import lax
from jax.sharding import PartitionSpec as P

CHUNKS = 2


def section_table(length, sign):
    index = jnp.arange(length, dtype=jnp.int32)
    angle = 2.0 * math.pi / length * (index[:, None] * index[None, :] % length).astype(jnp.float32)
    cos, sin = jnp.cos(angle), sign * jnp.sin(angle)
    return jnp.stack([jnp.stack([cos, sin], 1), jnp.stack([-sin, cos], 1)], 0)


def dft_tables(length, sign):
    first = 1 << (length.bit_length() - 1) // 2
    second = length // first
    index_a = jnp.arange(first, dtype=jnp.int32)
    index_b = jnp.arange(second, dtype=jnp.int32)
    angle = (
        2.0 * math.pi / length * (index_a[:, None] * index_b[None, :] % length).astype(jnp.float32)
    )
    twist = (jnp.cos(angle)[:, :, None], sign * jnp.sin(angle)[:, :, None])
    return first, second, section_table(first, sign), twist, section_table(second, sign)


def transform(parts, factors):
    first, second, table_one, (tw_cos, tw_sin), table_two = factors
    high = lax.Precision.HIGH
    cut = parts.reshape(2, first, second, parts.shape[2])
    step = jnp.einsum("pabk,paqc->qcbk", cut, table_one, precision=high)
    twisted = jnp.stack(
        [step[0] * tw_cos - step[1] * tw_sin, step[0] * tw_sin + step[1] * tw_cos], 0
    )
    return jnp.einsum("pcbk,pbqd->qdck", twisted, table_two, precision=high).reshape(parts.shape)


def per_device(anomalies, increment, spectrum, slabs):
    pairs, row_count, col_count = anomalies.shape[0] // 2, anomalies.shape[1], anomalies.shape[2]
    row_total, own_cols = spectrum.shape
    forward_y = dft_tables(col_count, -1.0)
    inverse_y = dft_tables(col_count, 1.0)
    forward_x = dft_tables(row_total, -1.0)
    inverse_x = dft_tables(row_total, 1.0)
    scaled = spectrum * (1.0 / (row_total * col_count))
    total = jnp.zeros_like(increment)
    width = own_cols // CHUNKS
    for pair in range(pairs):
        members = anomalies[2 * pair : 2 * pair + 2].astype(jnp.float32)
        fields = jnp.swapaxes(members * increment[None], 1, 2)
        waves = transform(fields, forward_y).reshape(2, slabs, own_cols, row_count)
        backs = []
        for chunk in range(CHUNKS):
            own = slice(chunk * width, (chunk + 1) * width)
            sent = lax.all_to_all(
                waves[:, :, own, :], "slab", split_axis=1, concat_axis=1, tiled=True
            )
            cols = sent.transpose(0, 1, 3, 2).reshape(2, row_total, width)
            cols = transform(cols, forward_x) * scaled[None, :, own]
            cols = transform(cols, inverse_x).reshape(2, slabs, row_count, width)
            back = cols.transpose(0, 1, 3, 2)
            backs.append(lax.all_to_all(back, "slab", split_axis=1, concat_axis=1, tiled=True))
        rows = jnp.concatenate(backs, 2).reshape(2, col_count, row_count)
        filtered = jnp.swapaxes(transform(rows, inverse_y), 1, 2)
        total = total + members[0] * filtered[0] + members[1] * filtered[1]
    return lax.psum(total, "mem")


def solution(mesh):
    placed = (P("mem", "slab", None), P("slab", None), P(None, "slab"))

    def body(anomalies, increment, spectrum):
        return per_device(anomalies, increment, spectrum, mesh.shape["slab"])

    return jax.shard_map(
        body, mesh=mesh, in_specs=placed, out_specs=P("slab", None), check_vma=False
    )
```

time: 1520 us -> 1290 us (0.85)
  matrix products: 521 us -> 181 us
  waiting for transfers between devices: 663 us -> 793 us
  local copies, waits for them, and re-layouts: 261 us -> 149 us
  other arithmetic: 33.7 us -> 117 us
    dot_general x32 -> x12, matrix products: 521 us -> 181 us  [the longest x6 91.9 us: transform(): step = jnp.einsum('pabk,paqc->qcbk', cut, table_one, precision=high)]
    all_to_all x4, waiting for transfers between devices: 511 us -> 641 us  [the longest x2 322 us: per_device(): lax.all_to_all(back, 'slab', split_axis=1, concat_axis=1, tiled=True)]
    reshape x4 -> x0, local copies, waits for them, and re-layouts: 91.1 us -> none  [the longest x2 45.6 us: transform(): out_real = out_real.reshape(shape)]
    dot_general x0 -> x4, local copies, waits for them, and re-layouts: none -> 43.7 us  [transform(): jnp.einsum('pcbk,pbqd->qdck', twisted, table_two, precision=high)]
    add x4 -> x0, local copies, waits for them, and re-layouts: 33.3 us -> none  [complex_section(): out_imag + jnp.einsum(form, imag_part, mat_cos, precision=highest)]
    sub x4 -> x0, local copies, waits for them, and re-layouts: 32.9 us -> none  [complex_section(): out_real - jnp.einsum(form, imag_part, mat_sin, precision=highest)]
    unnamed x38 -> x22, local copies, waits for them, and re-layouts: 51.5 us -> 21 us
    sub x0 -> x4, other arithmetic: none -> 30.1 us  [transform(): step[0] * tw_cos - step[1] * tw_sin]
  transfers between devices with their start and end apart: 5 -> 5, of which waited for: 5 -> 5; matrix products, arithmetic and copies ran while one was open for 14% -> 7% of each run, Pallas kernels for 0% -> 0%
where the time goes in v1:
time: 1290 us; the launch traced here: 1280 us
  waiting for transfers between devices  793 us (61%)
  matrix products  181 us (14%)
  local copies, waits for them, and re-layouts  149 us (12%)
  other arithmetic  117 us (9%)
  starting transfers between devices  22.7 us (2%)
  between operations  14.1 us (1%)
    all_to_all x2, waiting for transfers between devices, per_device(): lax.all_to_all(back, 'slab', split_axis=1, concat_axis=1, tiled=True)  322 us
    all_to_all x2, waiting for transfers between devices, per_device(): lax.all_to_all(waves[:, :, own, :], 'slab', split_axis=1, concat_axis=1,...  319 us
    psum x1, waiting for transfers between devices, per_device(): return lax.psum(total, 'mem')  152 us
    dot_general x6, matrix products, transform(): step = jnp.einsum('pabk,paqc->qcbk', cut, table_one, precision=high)  91.9 us
    dot_general x6, matrix products, transform(): jnp.einsum('pcbk,pbqd->qdck', twisted, table_two, precision=high)  89.2 us
    dot_general x4, local copies, waits for them, and re-layouts, transform(): jnp.einsum('pcbk,pbqd->qdck', twisted, table_two, precision=high)  43.7 us
    sub x4, other arithmetic, transform(): step[0] * tw_cos - step[1] * tw_sin  30.1 us
    another operation x6, other arithmetic, transform(): jnp.stack([step[0] * tw_cos - step[1] * tw_sin, step[0] * tw_sin + step[1...  28.6 us
  transfers between devices with their start and end apart: 5, of which 5 were waited for; matrix products, arithmetic and copies ran while one was open for 7% of the time, Pallas kernels for 0%

profile of v1, /device:TPU:0, one launch (start us, length us, event | category | flops | bytes accessed | tf_op | source)
XLA Modules:
  0.0 1277.0 jit_solution(5854949691891434646)
XLA Ops:
  6.5 0.1 broadcast_multiply_fusion.3
  6.7 0.1 fusion.97
  6.8 0.1 fusion.99
  7.0 0.1 broadcast_multiply_fusion.2
  7.1 0.0 copy-start.9
  7.1 12.0 copy.45
  19.1 8.9 copy.47
  28.1 12.1 broadcast_multiply_fusion
  40.2 0.7 fusion.80
  40.9 25.7 %fusion.34 = f32[2,64,64,512]{3,1,2,0:T(8,128)} fusion(f32[2,64,64,512]{3,2,1,0:T(8,128)} %bitcast.168, f32[1,64,2,64]{1,3,0,2:T(8,128)S(1)} %get-tuple-element.26, f32[1,64,2,64]{1,3,0,2:T(8,128)S(1)} %get-tuple-element.27), kind=kOutput, calls=%fused_computation.50 | convolution fusion | flops 3221241856 | bytes 33619968 | tf_op jit(solution)/shard_map/pabk,paqc->qcbk/dot_general | solution.py:34
  66.6 6.9 multiply_subtract_fusion.1
  73.5 6.2 pad_maximum_fusion
  79.7 25.8 %fusion.37 = f32[2,64,64,512]{3,1,2,0:T(8,128)} fusion(f32[2,64,64,512]{3,1,2,0:T(8,128)} %pad_maximum_fusion, f32[1,64,2,64]{1,3,0,2:T(8,128)S(1)} %get-tuple-element.26, f32[1,64,2,64]{1,3,0,2:T(8,128)S(1)} %get-tuple-element.27), kind=kOutput, calls=%fused_computation.51 | convolution fusion | flops 3221241856 | bytes 33619968 | tf_op jit(solution)/shard_map/pcbk,pbqd->qdck/dot_general | solution.py:38
  105.5 15.4 %copy.50 = f32[2,64,64,512]{3,2,1,0:T(8,128)S(1)} copy(f32[2,64,64,512]{3,1,2,0:T(8,128)} %fusion.37) | data formatting | bytes 33554432 | tf_op jit(solution)/shard_map/pcbk,pbqd->qdck/dot_general | solution.py:38
  121.0 7.0 fusion.106
  128.0 7.9 copy.61
  135.9 7.3 all-to-all-start.2
  143.3 8.0 copy.51
  151.3 175.2 %all-to-all-done.2 = f32[2,8,256,512]{3,2,0,1:T(8,128)} async-done(((f32[2,8,256,512]{3,2,0,1:T(8,128)}), f32[2,8,256,512]{3,2,0,1:T(8,128)}, u32[]{:S(2)}, u32[]{:S(2)}) %all-to-all-start.2) | async-done | bytes 8388640 | tf_op jit(solution)/shard_map/all_to_all | solution.py:58
  326.4 5.3 all-to-all-start
  331.7 4.4 broadcast_multiply_fusion.1
  336.2 0.7 fusion.107
  336.8 4.4 copy.65
  341.2 4.4 copy.55
  345.7 0.8 fusion.94
  346.4 9.1 copy.62
  355.5 14.7 %fusion.60 = f32[2,64,64,256]{3,1,2,0:T(8,128)} fusion(f32[2,64,64,256]{3,2,1,0:T(8,128)} %bitcast.172, f32[1,64,2,64]{1,3,0,2:T(8,128)S(1)} %get-tuple-element.26, f32[1,64,2,64]{1,3,0,2:T(8,128)S(1)} %get-tuple-element.27), kind=kOutput, calls=%fused_computation.69 | convolution fusion | flops 1610629120 | bytes 16842752 | tf_op jit(solution)/shard_map/pabk,paqc->qcbk/dot_general | solution.py:34
  370.3 143.7 %all-to-all-done = f32[2,8,256,512]{3,2,0,1:T(8,128)} async-done(((f32[2,8,256,512]{3,2,0,1:T(8,128)}), f32[2,8,256,512]{3,2,0,1:T(8,128)}, u32[]{:S(2)}, u32[]{:S(2)}) %all-to-all-start) | async-done | bytes 8388640 | tf_op jit(solution)/shard_map/all_to_all | solution.py:58
  514.0 8.7 copy.52
  522.6 12.4 fusion.54
  535.0 6.5 multiply_subtract_fusion.5
  541.6 4.1 maximum_bitcast_fusion.1
  545.7 8.4 fusion.18
  554.1 6.7 maximum_bitcast_fusion
  560.8 12.5 fusion.26
  573.4 6.0 fusion.51
  579.4 7.6 fusion.48
  586.9 9.7 multiply_subtract_fusion.4
  596.7 1.1 pad_maximum_fusion.3
  597.8 8.4 fusion.57
  606.2 5.3 copy.59
  611.5 3.8 copy.60
  615.3 5.0 all-to-all-start.1
  620.3 4.1 pad_maximum_fusion.4
  624.3 8.4 fusion.63
  632.7 5.0 copy.69
  637.8 4.0 copy.70
  641.7 160.5 %all-to-all-done.1 = f32[2,8,256,512]{2,3,0,1:T(8,128)} async-done(((f32[2,8,256,512]{2,3,0,1:T(8,128)}), f32[2,8,256,512]{2,3,0,1:T(8,128)}, u32[]{:S(2)}, u32[]{:S(2)}) %all-to-all-start.1) | async-done | bytes 8388640 | tf_op jit(solution)/shard_map/all_to_all | solution.py:65
  802.2 5.0 all-to-all-start.3
  807.3 0.0 all-reduce.2.cloned.1.call-start
  807.3 11.5 convert_element_type.112
  818.8 8.8 copy.71
  827.6 161.7 %all-to-all-done.3 = f32[2,8,256,512]{2,3,0,1:T(8,128)} async-done(((f32[2,8,256,512]{2,3,0,1:T(8,128)}), f32[2,8,256,512]{2,3,0,1:T(8,128)}, u32[]{:S(2)}, u32[]{:S(2)}) %all-to-all-start.3) | async-done | bytes 8388640 | tf_op jit(solution)/shard_map/all_to_all | solution.py:65
  989.3 8.7 copy.72
  998.0 11.6 pad_maximum_fusion.1
  1009.6 25.6 %fusion.40 = f32[2,64,64,512]{3,1,2,0:T(8,128)} fusion(f32[2,64,64,512]{3,2,1,0:T(8,128)} %bitcast.170, f32[1,64,2,64]{1,3,2,0:T(8,128)S(1)} %copy-done.3, f32[1,64,2,64]{1,3,2,0:T(8,128)S(1)} %copy-done.2), kind=kOutput, calls=%fused_computation.52 | convolution fusion | flops 3221241856 | bytes 33619968 | tf_op jit(solution)/shard_map/pabk,paqc->qcbk/dot_general | solution.py:34
  1035.2 6.9 multiply_subtract_fusion
  1042.1 6.4 pad_maximum_fusion.2
  1048.5 25.7 %fusion.43 = f32[2,64,64,512]{3,1,2,0:T(8,128)} fusion(f32[2,64,64,512]{3,1,2,0:T(8,128)} %pad_maximum_fusion.2, f32[1,64,2,64]{1,3,2,0:T(8,128)S(1)} %copy-done.3, f32[1,64,2,64]{1,3,2,0:T(8,128)S(1)} %copy-done.2), kind=kOutput, calls=%fused_computation.53 | convolution fusion | flops 3221241856 | bytes 33619968 | tf_op jit(solution)/shard_map/pcbk,pbqd->qdck/dot_general | solution.py:38
  1074.2 18.0 %copy.77 = f32[2,64,64,512]{3,2,1,0:T(8,128)} copy(f32[2,64,64,512]{3,1,2,0:T(8,128)} %fusion.43) | data formatting | bytes 33554432 | tf_op jit(solution)/shard_map/pcbk,pbqd->qdck/dot_general | solution.py:38
  1092.2 16.3 %fusion.13 = f32[512,4096]{0,1:T(8,128)} fusion(f32[2,512,4096]{1,2,0:T(8,128)} %bitcast.171, f32[2,512,4096]{1,2,0:T(8,128)} %convert_element_type.112), kind=kLoop, calls=%fused_computation.17 | loop fusion | flops 6291456 | bytes 41943040 | tf_op jit(solution)/shard_map/add | solution.py:68
  1108.4 0.0 all-reduce.2.cloned.1.call-update
  1108.5 152.3 %all-reduce.2.cloned.1.call-done = f32[512,4096]{0,1:T(8,128)} async-done(((f32[512,4096]{0,1:T(8,128)}), f32[512,4096]{0,1:T(8,128)}) %all-reduce.2.cloned.1.call-update) | async-done | bytes 8388624 | tf_op jit(solution)/shard_map/psum | solution.py:69
  1260.8 8.9 copy.78
  (19 shorter events, 0.0 us)
Async XLA Ops:
  7.1 59.4 %copy-start.9 = (f32[64,64]{0,1:T(8,128)}, f32[64,64]{0,1:T(8,128)S(1)}, u32[]{:S(2)}) copy-start(f32[64,64]{0,1:T(8,128)S(1)} %get-tuple-element.33) | copy-start | bytes 49156
  40.9 481.8 %copy-start.4 = (f32[1,64,2,64]{1,3,0,2:T(8,128)}, f32[1,64,2,64]{1,3,0,2:T(8,128)S(1)}, u32[]{:S(2)}) copy-start(f32[1,64,2,64]{1,3,0,2:T(8,128)S(1)} %get-tuple-element.26) | copy-start | bytes 98308
  40.9 481.8 %copy-start.6 = (f32[1,64,2,64]{1,3,0,2:T(8,128)}, f32[1,64,2,64]{1,3,0,2:T(8,128)S(1)}, u32[]{:S(2)}) copy-start(f32[1,64,2,64]{1,3,0,2:T(8,128)S(1)} %get-tuple-element.27) | copy-start | bytes 98308
  135.9 190.5 %all-to-all-start.2 = ((f32[2,8,256,512]{3,2,0,1:T(8,128)}), f32[2,8,256,512]{3,2,0,1:T(8,128)}, u32[]{:S(2)}, u32[]{:S(2)}) async-start(f32[2,8,256,512]{3,2,0,1:T(8,128)} %copy.61), calls=%async_computation.2 | async-start | bytes 16777216 | tf_op jit(solution)/shard_map/all_to_all | solution.py:58
  326.4 187.5 %all-to-all-start = ((f32[2,8,256,512]{3,2,0,1:T(8,128)}), f32[2,8,256,512]{3,2,0,1:T(8,128)}, u32[]{:S(2)}, u32[]{:S(2)}) async-start(f32[2,8,256,512]{3,2,0,1:T(8,128)} %copy.51), calls=%async_computation | async-start | bytes 16777216 | tf_op jit(solution)/shard_map/all_to_all | solution.py:58
  522.6 12.4 copy-start
  541.5 4.1 copy-start.5
  541.5 4.1 copy-start.7
  560.8 12.6 copy-start.1
  560.8 12.6 copy-start.2
  560.8 12.6 copy-start.3
  579.3 7.6 copy-start.8
  615.3 186.9 %all-to-all-start.1 = ((f32[2,8,256,512]{2,3,0,1:T(8,128)}), f32[2,8,256,512]{2,3,0,1:T(8,128)}, u32[]{:S(2)}, u32[]{:S(2)}) async-start(f32[2,8,256,512]{2,3,0,1:T(8,128)} %copy.60), calls=%async_computation.1 | async-start | bytes 16777216 | tf_op jit(solution)/shard_map/all_to_all | solution.py:65
  802.2 187.1 %all-to-all-start.3 = ((f32[2,8,256,512]{2,3,0,1:T(8,128)}), f32[2,8,256,512]{2,3,0,1:T(8,128)}, u32[]{:S(2)}, u32[]{:S(2)}) async-start(f32[2,8,256,512]{2,3,0,1:T(8,128)} %copy.70), calls=%async_computation.3 | async-start | bytes 16777216 | tf_op jit(solution)/shard_map/all_to_all | solution.py:65
  807.3 453.5 %all-reduce.2.cloned.1.call-start = ((), (), s32[]{:S(2)}) async-start(), calls=%async_computation.4 | async-start | bytes 16777216 | tf_op jit(solution)/shard_map/psum | solution.py:69
Sparse Core Ops, SparseCore 0:
  1108.6 152.1 all-reduce.1
